TPU v7x, 32 devices: a whole 2x2x4 slice. The times are simulated.
32 devices in a mesh: row: 8 (over y, x, core), col: 4 (over z).
Axes of the slice: x: 2, y: 2, z: 4, core: 2. Of those that a mesh axis runs over, the one named last changes fastest.
Arguments:
- record: float32 [2, 32768], P(None, ('row', 'col')), may hold values from -5 to 5
Outputs:
- spectrum: float32 [256, 256, 2, 2, 256], P('row', 'col')
All inputs are finite; a program needn't handle non-finite values.
Results may differ from a plain program's by a relative error of at most 0.00011.
Values sent between devices are 32-bit elements; how exact they have to be, the bound alone decides.
No kernel may reach another device: no remote copies, remote signals or barrier semaphores. Data moves between devices by JAX's collectives and lax.ppermute only.
A program may use at most 64 MiB of HBM per device.

v0:
```python
import math
import jax
import jax.numpy as jnp
from jax import lax
from jax.sharding import PartitionSpec as P

C = 256
P_SIZE = 256
HOP = 64
highest = lax.Precision.HIGHEST


def passed_along(block, axis, distance):
    devices = range(lax.axis_size(axis))
    route = [(i - distance, i) for i in devices if i - distance in devices]
    return lax.ppermute(block, axis, route)


def spectral_table(length, start_column, width, weights):
    position = jnp.arange(length, dtype=jnp.int32)
    column = start_column + jnp.arange(width, dtype=jnp.int32)
    turns = position[:, None] * column[None, :] % length
    phase = turns.astype(jnp.float32) * (2.0 * math.pi / length)
    cosine = weights[:, None] * jnp.cos(phase)
    sinus = weights[:, None] * jnp.sin(phase)
    upper = jnp.stack([cosine, -sinus], axis=1)
    bottom = jnp.stack([sinus, cosine], axis=1)
    return jnp.stack([upper, bottom], axis=0)


def hann_weights():
    position = jnp.arange(C, dtype=jnp.int32).astype(jnp.float32)
    return (0.5 - 0.5 * jnp.cos(position * (2.0 * math.pi / C))) / math.sqrt(3.0 * C / 8.0)


def framed(samples, amount):
    blocks = samples.reshape(2, amount + C // HOP - 1, HOP)
    return jnp.concatenate(
        [blocks[:, offset : offset + amount] for offset in range(C // HOP)], axis=2
    )


def downconvert(spectra, start_channel, start_frame):
    channel = start_channel + jnp.arange(spectra.shape[1], dtype=jnp.int32)
    moment = start_frame + jnp.arange(spectra.shape[2], dtype=jnp.int32)
    turns = (channel * HOP % C)[:, None] * (moment % C)[None, :] % C
    phase = turns.astype(jnp.float32) * (2.0 * math.pi / C)
    cosine = jnp.cos(phase)
    sinus = jnp.sin(phase)
    real_part = spectra[0] * cosine + spectra[1] * sinus
    imag_part = spectra[1] * cosine - spectra[0] * sinus
    return jnp.stack([real_part, imag_part])


def channelize(frames, start_channel, width, start_frame):
    weights = spectral_table(C, start_channel, width, hann_weights())
    spectra = lax.dot_general(
        weights,
        frames,
        (((0, 1), (0, 2)), ((), ())),
        precision=highest,
        preferred_element_type=jnp.float32,
    )
    return downconvert(spectra, start_channel, start_frame)


def correlate(leading, trailing):
    lead_count = leading.shape[1]
    trail_count = trailing.shape[1]
    windows = leading.shape[2] // P_SIZE
    lead = leading.reshape(2, lead_count, windows, P_SIZE)
    trail = trailing.reshape(2, trail_count, windows, P_SIZE)
    real_part = lead[0][:, None] * trail[0][None] + lead[1][:, None] * trail[1][None]
    imag_part = lead[1][:, None] * trail[0][None] - lead[0][:, None] * trail[1][None]
    weights = spectral_table(
        P_SIZE, 0, P_SIZE, jnp.full((P_SIZE,), 1.0 / math.sqrt(P_SIZE), jnp.float32)
    )
    real_table = weights[0].reshape(P_SIZE, 2 * P_SIZE)
    imag_table = weights[1].reshape(P_SIZE, 2 * P_SIZE)
    dims = (((3,), (0,)), ((), ()))
    result = lax.dot_general(
        real_part, real_table, dims, precision=highest, preferred_element_type=jnp.float32
    )
    result = result + lax.dot_general(
        imag_part, imag_table, dims, precision=highest, preferred_element_type=jnp.float32
    )
    return result.reshape(lead_count, trail_count, windows, 2, P_SIZE)


def local(record):
    row_count = lax.axis_size("row")
    col_count = lax.axis_size("col")
    lead_width = C // row_count
    trail_width = C // col_count
    own_frames = record.shape[1] // HOP
    device = lax.axis_index("row") * col_count + lax.axis_index("col")
    follow = passed_along(record[:, : C - HOP], ("row", "col"), -1)
    frames = framed(jnp.concatenate([record, follow], axis=1), own_frames)
    spectra = channelize(frames, 0, C, device * own_frames)
    shaped = spectra.reshape(2, C, 1, 1, own_frames)
    leading = lax.all_to_all(shaped, "row", split_axis=1, concat_axis=2, tiled=True)
    leading = lax.all_gather(leading, "col", axis=3, tiled=True)
    trailing = lax.all_to_all(shaped, "col", split_axis=1, concat_axis=3, tiled=True)
    trailing = lax.all_gather(trailing, "row", axis=2, tiled=True)
    leading = leading.reshape(2, lead_width, -1)
    trailing = trailing.reshape(2, trail_width, -1)
    return correlate(leading, trailing)


def solution(mesh):
    return jax.shard_map(
        local,
        mesh=mesh,
        in_specs=(P(None, ("row", "col")),),
        out_specs=P("row", "col", None, None, None),
        check_vma=False,
    )
```

profile of v0, /device:TPU:0, one launch (start us, length us, event | category | flops | bytes accessed | tf_op | source)
XLA Modules:
  0.0 90.0 jit_solution(8008926294532363169)
XLA Ops:
  0.0 0.7 slice.43
  0.7 1.3 %collective-permute-start = (f32[2,192]{1,0:T(2,128)S(1)}, f32[2,192]{1,0:T(2,128)S(1)}, u32[]{:S(2)}, u32[]{:S(2)}) collective-permute-start(f32[2,192]{1,0:T(2,128)S(1)} %slice.43), channel_id=1, source_target_pairs={{1,0},{2,1},{3,2},{4,3},{5,4},{6,5},{7,6},{8,7},{9,8},{10,9},{11,1... | collective-permute-start | bytes 4616 | tf_op jit(solution)/shard_map/ppermute | solution.py:16
  2.0 1.0 %fusion.32 = f32[256,1,256]{2,0,1:T(8,128)S(1)} fusion(), kind=kLoop, calls=%fused_computation.40 | loop fusion | flops 1048576 | bytes 262144 | tf_op jit(solution)/shard_map/neg | solution.py:26
  3.0 1.1 %broadcast_multiply_fusion = (f32[256,1,256]{2,0,1:T(8,128)S(1)}, f32[256,1,256]{2,0,1:T(8,128)S(1)}) fusion(), kind=kLoop, calls=%fused_computation.34 | loop fusion | flops 1048576 | bytes 524288 | tf_op jit(solution)/shard_map/mul;broadcast_in_dim;broadcast_in_dim | solution.py:25
  4.1 1.1 %fusion.33 = (f32[256,1,256]{2,0,1:T(8,128)S(1)}, f32[256,1,256]{2,0,1:T(8,128)S(1)}, f32[256,1,256]{2,0,1:T(8,128)S(1)}) fusion(f32[256]{0:T(256)S(1)} %subtract_multiply_fusion), kind=kLoop, calls=%fused_computation.41 | loop fusion | flops 1114112 | bytes 787456 | tf_op jit(solution)/shard_map/neg | solution.py:26
  5.3 1.9 %collective-permute-done = f32[2,192]{1,0:T(2,128)S(1)} collective-permute-done((f32[2,192]{1,0:T(2,128)S(1)}, f32[2,192]{1,0:T(2,128)S(1)}, u32[]{:S(2)}, u32[]{:S(2)}) %collective-permute-start) | collective-permute-done | bytes 1568 | tf_op jit(solution)/shard_map/ppermute | solution.py:16
  7.2 0.7 pad_maximum_fusion.2
  8.0 0.7 convolution_bitcast_fusion
  8.7 0.2 multiply_add_fusion
  8.8 0.1 copy.17
  9.0 0.9 %reshape.367 = f32[8,1,1024]{2,1,0:T(1,128)} reshape(f32[256,1,1,2,16]{4,3,2,1,0:T(2,128)S(1)} %bitcast.38) | data formatting | bytes 65536
  9.9 7.2 %all-to-all-start = ((f32[8,1,1024]{2,1,0:T(1,128)}), f32[8,1,1024]{2,1,0:T(1,128)S(1)}, u32[]{:S(2)}, u32[]{:S(2)}) async-start(f32[8,1,1024]{2,1,0:T(1,128)} %reshape.367), calls=%async_computation | async-start | bytes 65536 | tf_op jit(solution)/shard_map/all_to_all | solution.py:101
  17.2 0.2 copy.25
  17.4 0.2 copy.27
  17.7 0.9 %reshape.365 = f32[4,1,2048]{2,1,0:T(1,128)} reshape(f32[256,1,1,2,16]{4,3,2,1,0:T(2,128)S(1)} %bitcast.39) | data formatting | bytes 65536
  18.6 3.4 %all-to-all-done = f32[8,1,1024]{2,1,0:T(1,128)S(1)} async-done(((f32[8,1,1024]{2,1,0:T(1,128)}), f32[8,1,1024]{2,1,0:T(1,128)S(1)}, u32[]{:S(2)}, u32[]{:S(2)}) %all-to-all-start) | async-done | bytes 32800 | tf_op jit(solution)/shard_map/all_to_all | solution.py:101
  22.0 3.3 %all-to-all-start.1 = ((f32[4,1,2048]{2,1,0:T(1,128)}), f32[4,1,2048]{2,1,0:T(1,128)S(1)}, u32[]{:S(2)}, u32[]{:S(2)}) async-start(f32[4,1,2048]{2,1,0:T(1,128)} %reshape.365), calls=%async_computation.1 | async-start | bytes 65536 | tf_op jit(solution)/shard_map/all_to_all | solution.py:103
  25.3 0.5 broadcast.533
  25.8 0.6 reduce.1
  26.4 0.4 reshape.368
  26.8 0.1 copy.18
  27.0 15.8 %all-gather = f32[2,32,8,4,1,16]{1,5,3,2,4,0:T(8,128)S(1)} all-gather(f32[2,32,8,1,1,16]{1,5,3,2,4,0:T(8,128)S(1)} %bitcast.48), channel_id=2, replica_groups=mesh['row'=8,'col'=4] {'col'}, dimensions={3}, use_global_device_ids=true | all-gather | bytes 163840 | tf_op jit(solution)/shard_map/all_gather | solution.py:102
  42.9 0.1 copy.23
  43.0 0.6 reduce
  43.7 0.4 reshape.366
  44.1 0.1 copy.21
  44.2 9.2 %all-gather.1 = f32[2,64,8,4,1,16]{1,5,3,2,4,0:T(8,128)S(1)} all-gather(f32[2,64,1,4,1,16]{1,5,3,2,4,0:T(8,128)S(1)} %bitcast.49), channel_id=3, replica_groups=mesh['row'=8,'col'=4] {'row'}, dimensions={2}, use_global_device_ids=true | all-gather | bytes 294912 | tf_op jit(solution)/shard_map/all_gather | solution.py:104
  53.5 0.1 copy.22
  53.7 7.9 %fusion = f32[32,64,2,512]{3,1,2,0:T(8,128)S(1)} fusion(f32[256,512,1,1]{0,1,3,2:T(8,128)S(1)} %bitcast.41, f32[64,2,256]{2,0,1:T(8,128)S(1)} %copy.24, f32[32,2,256]{2,1,0:T(2,128)S(1)} %copy.23, f32[64,2,256]{2,0,1:T(8,128)S(1)} %copy.22, f32[32,2,256]{2,1,0:T(2,128)S(1)} %copy.19), kind=kOutput, calls=%fused_computation | convolution fusion | flops 6445596672 | bytes 9306112 | tf_op jit(solution)/shard_map/dot_general | solution.py:84
  61.6 9.8 %fusion.8 = f32[32,64,2,512]{3,1,2,0:T(8,128)} fusion(f32[32,64,2,512]{3,1,2,0:T(8,128)S(1)} %fusion, f32[256,512,1,1]{0,1,3,2:T(8,128)S(1)} %bitcast.40, f32[64,2,256]{2,0,1:T(8,128)S(1)} %copy.24, f32[32,2,256]{2,1,0:T(2,128)S(1)} %copy.23, f32[64,2,256]{2,0,1:T(8,128)S(1)} %copy.22, f32[32,2,256]{2,1,0:T(2,128)S(1)} %copy.19), kind=kOutput, calls=%fused_computation.8 | convolution fusion | flops 6447693824 | bytes 17694720 | tf_op jit(solution)/shard_map/dot_general | solution.py:81
  71.4 10.6 %reshape.350 = f32[32,64,2,2,256]{4,3,1,2,0:T(2,128)} reshape(f32[32,64,2,512]{3,1,2,0:T(8,128)} %fusion.8) | data formatting | bytes 16777216 | tf_op jit(solution)/shard_map/reshape | solution.py:87
  81.9 8.0 %copy.29 = f32[32,64,2,2,256]{4,3,2,1,0:T(2,128)} copy(f32[32,64,2,2,256]{4,3,1,2,0:T(2,128)} %reshape.350) | data formatting | bytes 16777216 | tf_op jit(solution)/shard_map/reshape | solution.py:87
  (13 shorter events, 0.6 us)
Async XLA Ops:
  0.7 6.5 %collective-permute-start = (f32[2,192]{1,0:T(2,128)S(1)}, f32[2,192]{1,0:T(2,128)S(1)}, u32[]{:S(2)}, u32[]{:S(2)}) collective-permute-start(f32[2,192]{1,0:T(2,128)S(1)} %slice.43), channel_id=1, source_target_pairs={{1,0},{2,1},{3,2},{4,3},{5,4},{6,5},{7,6},{8,7},{9,8},{10,9},{11,1... | collective-permute-start | bytes 4616 | tf_op jit(solution)/shard_map/ppermute | solution.py:16
  9.9 12.1 %all-to-all-start = ((f32[8,1,1024]{2,1,0:T(1,128)}), f32[8,1,1024]{2,1,0:T(1,128)S(1)}, u32[]{:S(2)}, u32[]{:S(2)}) async-start(f32[8,1,1024]{2,1,0:T(1,128)} %reshape.367), calls=%async_computation | async-start | bytes 65536 | tf_op jit(solution)/shard_map/all_to_all | solution.py:101
  22.0 21.0 %all-to-all-start.1 = ((f32[4,1,2048]{2,1,0:T(1,128)}), f32[4,1,2048]{2,1,0:T(1,128)S(1)}, u32[]{:S(2)}, u32[]{:S(2)}) async-start(f32[4,1,2048]{2,1,0:T(1,128)} %reshape.365), calls=%async_computation.1 | async-start | bytes 65536 | tf_op jit(solution)/shard_map/all_to_all | solution.py:103
where the time goes:
time: 90.7 us; the launch traced here: 90 us
  blocking collectives  25 us (28%)
  local copies, waits for them, and re-layouts  23.8 us (26%)
  matrix products  18.3 us (20%)
  starting transfers between devices  11.8 us (13%)
  other arithmetic  5.47 us (6%)
  waiting for transfers between devices  5.31 us (6%)
    reshape x2, local copies, waits for them, and re-layouts, correlate(): return result.reshape(lead_count, trail_count, windows, 2, P_SIZE)  18.6 us
    all_gather x1, blocking collectives, local(): leading = lax.all_gather(leading, 'col', axis=3, tiled=True)  15.8 us
    dot_general x1, matrix products, correlate(): lax.dot_general(real_part, real_table, dims, precision=highest, preferred...  9.76 us
    all_gather x1, blocking collectives, local(): trailing = lax.all_gather(trailing, 'row', axis=2, tiled=True)  9.23 us
    dot_general x1, matrix products, correlate(): lax.dot_general(imag_part, imag_table, dims, precision=highest, preferred...  7.91 us
    all_to_all x1, starting transfers between devices, local(): lax.all_to_all(shaped, 'row', split_axis=1, concat_axis=2, tiled=True)  7.24 us
    all_to_all x1, waiting for transfers between devices, local(): lax.all_to_all(shaped, 'row', split_axis=1, concat_axis=2, tiled=True)  3.4 us
    all_to_all x1, starting transfers between devices, local(): lax.all_to_all(shaped, 'col', split_axis=1, concat_axis=3, tiled=True)  3.3 us
  transfers between devices with their start and end apart: 3, of which 2 were waited for; matrix products, arithmetic and copies ran while one was open for 7% of the time, Pallas kernels for 0%

commit v1 on v0

--- a/solution.py
+++ b/solution.py
@@ -8,6 +8,17 @@
 P_SIZE = 256
 HOP = 64
 highest = lax.Precision.HIGHEST
+
+
+def turned_line(x, mesh_axis, along):
+    count = lax.axis_size(mesh_axis)
+    right = [(i, (i + 1) % count) for i in range(count)]
+    parts = [x]
+    for stride in range(1, count):
+        parts = [lax.ppermute(parts[0], mesh_axis, right), *parts]
+    whole = jnp.concatenate(parts, axis=along)
+    turn = (lax.axis_index(mesh_axis) + 1) * parts[-1].shape[along]
+    return jnp.roll(whole, turn, axis=along)
 
 
 def passed_along(block, axis, distance):
@@ -101,7 +112,7 @@
     leading = lax.all_to_all(shaped, "row", split_axis=1, concat_axis=2, tiled=True)
     leading = lax.all_gather(leading, "col", axis=3, tiled=True)
     trailing = lax.all_to_all(shaped, "col", split_axis=1, concat_axis=3, tiled=True)
-    trailing = lax.all_gather(trailing, "row", axis=2, tiled=True)
+    trailing = turned_line(trailing, "row", 2)
     leading = leading.reshape(2, lead_width, -1)
     trailing = trailing.reshape(2, trail_width, -1)
     return correlate(leading, trailing)

time: 90.7 us -> 107 us (1.18)
  waiting for transfers between devices: 5.31 us -> 24.9 us
  starting transfers between devices: 11.8 us -> 5.87 us
  blocking collectives: 25 us -> 28.2 us
    ppermute x0 -> x7, waiting for transfers between devices: none -> 17 us  [turned_line(): parts = [lax.ppermute(parts[0], mesh_axis, right), *parts]]
    all_to_all x0 -> x1, blocking collectives: none -> 12 us  [local(): lax.all_to_all(shaped, 'col', split_axis=1, concat_axis=3, tiled=True)]
    all_gather x1 -> x0, blocking collectives: 9.23 us -> none  [local(): trailing = lax.all_gather(trailing, 'row', axis=2, tiled=True)]
    all_to_all x1 -> x0, starting transfers between devices: 3.3 us -> none  [local(): lax.all_to_all(shaped, 'col', split_axis=1, concat_axis=3, tiled=True)]
    all_to_all x1, starting transfers between devices: 7.24 us -> 3.97 us  [local(): lax.all_to_all(shaped, 'row', split_axis=1, concat_axis=2, tiled=True)]
    ppermute x1, waiting for transfers between devices: 1.91 us -> 3.95 us  [passed_along(): return lax.ppermute(block, axis, route)]
    unnamed x4 -> x19, local copies, waits for them, and re-layouts: 2.65 us -> 2.15 us
  transfers between devices with their start and end apart: 3 -> 9, of which waited for: 2 -> 6; matrix products, arithmetic and copies ran while one was open for 7% -> 6% of each run, Pallas kernels for 0% -> 0%
where the time goes in v1:
time: 107 us
  blocking collectives  28.2 us (26%)
  waiting for transfers between devices  24.9 us (23%)
  local copies, waits for them, and re-layouts  23.4 us (22%)
  matrix products  18.3 us (17%)
  starting transfers between devices  5.87 us (5%)
  other arithmetic  5.62 us (5%)
    reshape x2, local copies, waits for them, and re-layouts, correlate(): return result.reshape(lead_count, trail_count, windows, 2, P_SIZE)  18.6 us
    ppermute x7, waiting for transfers between devices, turned_line(): parts = [lax.ppermute(parts[0], mesh_axis, right), *parts]  17 us
    all_gather x1, blocking collectives, local(): leading = lax.all_gather(leading, 'col', axis=3, tiled=True)  16.2 us
    all_to_all x1, blocking collectives, local(): lax.all_to_all(shaped, 'col', split_axis=1, concat_axis=3, tiled=True)  12 us
    dot_general x1, matrix products, correlate(): lax.dot_general(real_part, real_table, dims, precision=highest, preferred...  9.75 us
    dot_general x1, matrix products, correlate(): lax.dot_general(imag_part, imag_table, dims, precision=highest, preferred...  7.91 us
    all_to_all x1, waiting for transfers between devices, local(): lax.all_to_all(shaped, 'row', split_axis=1, concat_axis=2, tiled=True)  3.99 us
    all_to_all x1, starting transfers between devices, local(): lax.all_to_all(shaped, 'row', split_axis=1, concat_axis=2, tiled=True)  3.97 us
  transfers between devices with their start and end apart: 9, of which 6 were waited for; matrix products, arithmetic and copies ran while one was open for 6% of the time, Pallas kernels for 0%

profile of v1, /device:TPU:0, one launch (start us, length us, event | category | flops | bytes accessed | tf_op | source)
XLA Modules:
  0.0 106.8 jit_solution(7558239780874186439)
XLA Ops:
  0.0 0.7 slice.43
  0.7 1.3 %collective-permute-start = (f32[2,192]{1,0:T(2,128)S(1)}, f32[2,192]{1,0:T(2,128)S(1)}, u32[]{:S(2)}, u32[]{:S(2)}) collective-permute-start(f32[2,192]{1,0:T(2,128)S(1)} %slice.43), channel_id=1, source_target_pairs={{1,0},{2,1},{3,2},{4,3},{5,4},{6,5},{7,6},{8,7},{9,8},{10,9},{11,1... | collective-permute-start | bytes 4616 | tf_op jit(solution)/shard_map/ppermute | solution.py:27
  2.0 1.1 %fusion.33 = (f32[256,1,256]{2,0,1:T(8,128)S(1)}, f32[256,1,256]{2,0,1:T(8,128)S(1)}, f32[256,1,256]{2,0,1:T(8,128)S(1)}) fusion(f32[256]{0:T(256)S(1)} %subtract_multiply_fusion), kind=kLoop, calls=%fused_computation.41 | loop fusion | flops 1114112 | bytes 787456 | tf_op jit(solution)/shard_map/neg | solution.py:37
  3.2 4.0 %collective-permute-done = f32[2,192]{1,0:T(2,128)S(1)} collective-permute-done((f32[2,192]{1,0:T(2,128)S(1)}, f32[2,192]{1,0:T(2,128)S(1)}, u32[]{:S(2)}, u32[]{:S(2)}) %collective-permute-start) | collective-permute-done | bytes 1568 | tf_op jit(solution)/shard_map/ppermute | solution.py:27
  7.2 0.7 pad_maximum_fusion.2
  8.0 0.7 convolution_bitcast_fusion
  8.7 0.2 multiply_add_fusion
  8.8 0.1 copy.17
  9.0 0.3 reshape.360
  9.3 12.0 %all_to_all.36 = f32[4,1,2048]{2,1,0:T(1,128)S(1)} all-to-all(f32[4,1,2048]{2,1,0:T(1,128)S(1)} %reshape.360), channel_id=1, replica_groups=mesh['row'=8,'col'=4] {'col'}, dimensions={0} | all-to-all | bytes 65536 | tf_op jit(solution)/shard_map/all_to_all | solution.py:114
  21.3 0.5 broadcast.534
  21.8 0.7 reduce
  22.6 0.4 reshape.361
  23.1 4.6 %collective-permute-done.1 = f32[2,64,1,4,16]{1,4,3,2,0:T(8,128)S(1)} collective-permute-done((f32[2,64,1,4,16]{1,4,3,2,0:T(8,128)S(1)}, f32[2,64,1,4,16]{1,4,3,2,0:T(8,128)S(1)}, u32[]{:S(2)}, u32[]{:S(2)}) %collective-permute-start.1) | collective-permute-done | bytes 32800 | tf_op jit(solution)/shard_map/ppermute | solution.py:18
  27.7 4.6 %collective-permute-done.2 = f32[2,64,1,4,16]{1,4,3,2,0:T(8,128)S(1)} collective-permute-done((f32[2,64,1,4,16]{1,4,3,2,0:T(8,128)S(1)}, f32[2,64,1,4,16]{1,4,3,2,0:T(8,128)S(1)}, u32[]{:S(2)}, u32[]{:S(2)}) %collective-permute-start.2) | collective-permute-done | bytes 32800 | tf_op jit(solution)/shard_map/ppermute | solution.py:18
  32.3 1.1 broadcast_multiply_fusion
  33.4 3.5 %collective-permute-done.3 = f32[2,64,1,4,16]{1,4,3,2,0:T(8,128)S(1)} collective-permute-done((f32[2,64,1,4,16]{1,4,3,2,0:T(8,128)S(1)}, f32[2,64,1,4,16]{1,4,3,2,0:T(8,128)S(1)}, u32[]{:S(2)}, u32[]{:S(2)}) %collective-permute-start.3) | collective-permute-done | bytes 32800 | tf_op jit(solution)/shard_map/ppermute | solution.py:18
  36.9 1.0 fusion.32
  37.9 1.0 reshape.362
  38.8 4.0 %all-to-all-start = ((f32[8,1,1024]{2,1,0:T(1,128)}), f32[8,1,1024]{2,1,0:T(1,128)S(1)}, u32[]{:S(2)}, u32[]{:S(2)}) async-start(f32[8,1,1024]{2,1,0:T(1,128)} %reshape.362), calls=%async_computation | async-start | bytes 65536 | tf_op jit(solution)/shard_map/all_to_all | solution.py:112
  42.8 0.5 collective-permute-start.5
  43.4 0.2 copy.25
  43.6 0.2 copy.27
  43.8 4.0 %all-to-all-done = f32[8,1,1024]{2,1,0:T(1,128)S(1)} async-done(((f32[8,1,1024]{2,1,0:T(1,128)}), f32[8,1,1024]{2,1,0:T(1,128)S(1)}, u32[]{:S(2)}, u32[]{:S(2)}) %all-to-all-start) | async-done | bytes 32800 | tf_op jit(solution)/shard_map/all_to_all | solution.py:112
  47.8 0.7 reduce.1
  48.5 0.4 reshape.363
  49.1 16.2 %all-gather = f32[2,32,8,4,1,16]{1,5,3,2,4,0:T(8,128)S(1)} all-gather(f32[2,32,8,1,1,16]{1,5,3,2,4,0:T(8,128)S(1)} %bitcast.53), channel_id=2, replica_groups=mesh['row'=8,'col'=4] {'col'}, dimensions={3}, use_global_device_ids=true | all-gather | bytes 163840 | tf_op jit(solution)/shard_map/all_gather | solution.py:113
  65.7 4.3 %collective-permute-done.7 = f32[2,64,1,4,16]{1,4,3,2,0:T(8,128)S(1)} collective-permute-done((f32[2,64,1,4,16]{1,4,3,2,0:T(8,128)S(1)}, f32[2,64,1,4,16]{1,4,3,2,0:T(8,128)S(1)}, u32[]{:S(2)}, u32[]{:S(2)}) %collective-permute-start.7) | collective-permute-done | bytes 32800 | tf_op jit(solution)/shard_map/ppermute | solution.py:18
  70.5 7.9 %fusion = f32[32,64,2,512]{3,1,2,0:T(8,128)S(1)} fusion(f32[256,512,1,1]{0,1,3,2:T(8,128)S(1)} %bitcast.45, f32[64,2,256]{2,0,1:T(8,128)S(1)} %copy.24, f32[32,2,256]{2,1,0:T(2,128)S(1)} %copy.23, f32[64,2,256]{2,0,1:T(8,128)S(1)} %copy.22, f32[32,2,256]{2,1,0:T(2,128)S(1)} %copy.19), kind=kOutput, calls=%fused_computation | convolution fusion | flops 6445596672 | bytes 9306112 | tf_op jit(solution)/shard_map/dot_general | solution.py:95
  78.4 9.8 %fusion.8 = f32[32,64,2,512]{3,1,2,0:T(8,128)} fusion(f32[32,64,2,512]{3,1,2,0:T(8,128)S(1)} %fusion, f32[256,512,1,1]{0,1,3,2:T(8,128)S(1)} %bitcast.44, f32[64,2,256]{2,0,1:T(8,128)S(1)} %copy.24, f32[32,2,256]{2,1,0:T(2,128)S(1)} %copy.23, f32[64,2,256]{2,0,1:T(8,128)S(1)} %copy.22, f32[32,2,256]{2,1,0:T(2,128)S(1)} %copy.19), kind=kOutput, calls=%fused_computation.8 | convolution fusion | flops 6447693824 | bytes 17694720 | tf_op jit(solution)/shard_map/dot_general | solution.py:92
  88.2 10.6 %reshape.350 = f32[32,64,2,2,256]{4,3,1,2,0:T(2,128)} reshape(f32[32,64,2,512]{3,1,2,0:T(8,128)} %fusion.8) | data formatting | bytes 16777216 | tf_op jit(solution)/shard_map/reshape | solution.py:98
  98.7 8.0 %copy.29 = f32[32,64,2,2,256]{4,3,2,1,0:T(2,128)} copy(f32[32,64,2,2,256]{4,3,1,2,0:T(2,128)} %reshape.350) | data formatting | bytes 16777216 | tf_op jit(solution)/shard_map/reshape | solution.py:98
  (41 shorter events, 1.3 us)
Async XLA Ops:
  0.7 6.5 %collective-permute-start = (f32[2,192]{1,0:T(2,128)S(1)}, f32[2,192]{1,0:T(2,128)S(1)}, u32[]{:S(2)}, u32[]{:S(2)}) collective-permute-start(f32[2,192]{1,0:T(2,128)S(1)} %slice.43), channel_id=1, source_target_pairs={{1,0},{2,1},{3,2},{4,3},{5,4},{6,5},{7,6},{8,7},{9,8},{10,9},{11,1... | collective-permute-start | bytes 4616 | tf_op jit(solution)/shard_map/ppermute | solution.py:27
  23.1 4.6 %collective-permute-start.1 = (f32[2,64,1,4,16]{1,4,3,2,0:T(8,128)S(1)}, f32[2,64,1,4,16]{1,4,3,2,0:T(8,128)S(1)}, u32[]{:S(2)}, u32[]{:S(2)}) collective-permute-start(f32[2,64,1,4,16]{1,4,3,2,0:T(8,128)S(1)} %bitcast.52), channel_id=1, source_target_pairs={{0,4},{4,8},{8,12},{12,16},{16,20},{20,24},{24,28},{28,0},{1,5},{5... | collective-permute-start | bytes 98312 | tf_op jit(solution)/shard_map/ppermute | solution.py:18
  27.7 4.6 %collective-permute-start.2 = (f32[2,64,1,4,16]{1,4,3,2,0:T(8,128)S(1)}, f32[2,64,1,4,16]{1,4,3,2,0:T(8,128)S(1)}, u32[]{:S(2)}, u32[]{:S(2)}) collective-permute-start(f32[2,64,1,4,16]{1,4,3,2,0:T(8,128)S(1)} %collective-permute-done.1), channel_id=1, source_target_pairs={{0,4},{4,8},{8,12},{12,16},{16,20},{20,24},{24,28},{28,0},{1,5},{5... | collective-permute-start | bytes 98312 | tf_op jit(solution)/shard_map/ppermute | solution.py:18
  32.3 4.6 %collective-permute-start.3 = (f32[2,64,1,4,16]{1,4,3,2,0:T(8,128)S(1)}, f32[2,64,1,4,16]{1,4,3,2,0:T(8,128)S(1)}, u32[]{:S(2)}, u32[]{:S(2)}) collective-permute-start(f32[2,64,1,4,16]{1,4,3,2,0:T(8,128)S(1)} %collective-permute-done.2), channel_id=1, source_target_pairs={{0,4},{4,8},{8,12},{12,16},{16,20},{20,24},{24,28},{28,0},{1,5},{5... | collective-permute-start | bytes 98312 | tf_op jit(solution)/shard_map/ppermute | solution.py:18
  36.9 5.9 %collective-permute-start.4 = (f32[2,64,1,4,16]{1,4,3,2,0:T(8,128)S(1)}, f32[2,64,1,4,16]{1,4,3,2,0:T(8,128)S(1)}, u32[]{:S(2)}, u32[]{:S(2)}) collective-permute-start(f32[2,64,1,4,16]{1,4,3,2,0:T(8,128)S(1)} %collective-permute-done.3), channel_id=1, source_target_pairs={{0,4},{4,8},{8,12},{12,16},{16,20},{20,24},{24,28},{28,0},{1,5},{5... | collective-permute-start | bytes 98312 | tf_op jit(solution)/shard_map/ppermute | solution.py:18
  38.8 9.0 %all-to-all-start = ((f32[8,1,1024]{2,1,0:T(1,128)}), f32[8,1,1024]{2,1,0:T(1,128)S(1)}, u32[]{:S(2)}, u32[]{:S(2)}) async-start(f32[8,1,1024]{2,1,0:T(1,128)} %reshape.362), calls=%async_computation | async-start | bytes 65536 | tf_op jit(solution)/shard_map/all_to_all | solution.py:112
  42.8 6.3 %collective-permute-start.5 = (f32[2,64,1,4,16]{1,4,3,2,0:T(8,128)S(1)}, f32[2,64,1,4,16]{1,4,3,2,0:T(8,128)S(1)}, u32[]{:S(2)}, u32[]{:S(2)}) collective-permute-start(f32[2,64,1,4,16]{1,4,3,2,0:T(8,128)S(1)} %collective-permute-done.4), channel_id=1, source_target_pairs={{0,4},{4,8},{8,12},{12,16},{16,20},{20,24},{24,28},{28,0},{1,5},{5... | collective-permute-start | bytes 98312 | tf_op jit(solution)/shard_map/ppermute | solution.py:18
  49.1 16.3 %collective-permute-start.6 = (f32[2,64,1,4,16]{1,4,3,2,0:T(8,128)S(1)}, f32[2,64,1,4,16]{1,4,3,2,0:T(8,128)S(1)}, u32[]{:S(2)}, u32[]{:S(2)}) collective-permute-start(f32[2,64,1,4,16]{1,4,3,2,0:T(8,128)S(1)} %collective-permute-done.5), channel_id=1, source_target_pairs={{0,4},{4,8},{8,12},{12,16},{16,20},{20,24},{24,28},{28,0},{1,5},{5... | collective-permute-start | bytes 98312 | tf_op jit(solution)/shard_map/ppermute | solution.py:18
  65.4 4.6 %collective-permute-start.7 = (f32[2,64,1,4,16]{1,4,3,2,0:T(8,128)S(1)}, f32[2,64,1,4,16]{1,4,3,2,0:T(8,128)S(1)}, u32[]{:S(2)}, u32[]{:S(2)}) collective-permute-start(f32[2,64,1,4,16]{1,4,3,2,0:T(8,128)S(1)} %collective-permute-done.6), channel_id=1, source_target_pairs={{0,4},{4,8},{8,12},{12,16},{16,20},{20,24},{24,28},{28,0},{1,5},{5... | collective-permute-start | bytes 98312 | tf_op jit(solution)/shard_map/ppermute | solution.py:18
